TPU v7x, 32 devices: a whole 2x2x4 slice. The times are simulated.
32 devices in a mesh: freq: 16 (over z, y, x), depth: 2 (over core).
Axes of the slice: x: 2, y: 2, z: 4, core: 2. Of those that a mesh axis runs over, the one named last changes fastest.
Arguments:
- pressure_field: bfloat16 [8192, 4096], P('depth', 'freq'), may hold values from -6 to 6
- block_main: bfloat16 [8192, 3, 2, 128], P('depth'), may hold values from -0.15625 to 0.15625
- block_coupled: bfloat16 [8192, 3, 2, 128], P('depth'), may hold values from -0.15625 to 0.15625
- coupling: float32 [4096], P('freq'), may hold values from -3 to 3
- frequencies: float32 [2048], replicated, may hold values from 1 to 1024
- receivers: int32 [512], replicated, may hold values from 0 to 8191
- floors: int32 [4], replicated, may hold values from 2048 to 8191
Outputs:
- series: float32 [512, 2048], P('depth', 'freq')
Inputs may be any that keep to these rules, and one draw needn't show every extreme that they name: `receivers`: any depth cells, repeats possible.
All inputs are finite; a program needn't handle non-finite values.
Results may differ from a plain program's by a relative error of at most 0.0061.
Values may be sent and summed in bfloat16 or wider, within the bound.
A program may use at most 256 MiB of HBM per device.

v0:
```python
import functools
import math

import jax
import jax.numpy as jnp
from jax import lax
from jax.experimental import pallas as pl
from jax.experimental.pallas import tpu as pltpu
from jax.sharding import PartitionSpec as P

NT = 2048
STEPS = 4

COS_TERMS = (1.0, -19.739208221435547, 64.93939208984375, -85.45665740966797,
             60.242130279541016, -26.4046688079834, 7.800131320953369, -1.453112244606018)
SIN_TERMS = (6.2831854820251465, -41.34170150756836, 81.6052474975586, -76.70580291748047,
             42.05775451660156, -15.086565017700195, 3.7813189029693604, -0.6207787394523621)

MESH = pl.DeviceIdType.MESH
F32 = jnp.float32
BF16 = jnp.bfloat16


def poly(terms, z):
    total = jnp.full_like(z, terms[-1])
    for term in terms[-2::-1]:
        total = total * z + F32(term)
    return total


def unroll_of(count, choices=(5, 4, 3, 2, 1)):
    return next(c for c in choices if count % c == 0)


def split_rows(rows, parts):
    unit = 16
    units = rows // unit
    cuts = [round(units * i / parts) * unit for i in range(parts)] + [rows]
    return [(cuts[i], cuts[i + 1] - cuts[i]) for i in range(parts)]


def plan_of(rows, bits):
    parts = min(3, max(1, bits - 1))
    plan = []
    for i, (start, count) in enumerate(split_rows(rows, parts)):
        low = list(range(bits - 1))
        order = low[i:] + low[:i] + [bits - 1]
        plan.append((start, count, order))
    return plan


def kernel(depth_n, freq_n, bits, factor, plan,
           field, main_hbm, side_hbm, weights, freqs, receivers, floors, out,
           raw_main, raw_side, spread, ops, w_buf, final, halo, picked, owned, pick_in,
           basis, sums, *rest):
    n_parts = len(plan)
    send_bufs = rest[:n_parts]
    recv_bufs = rest[n_parts:2 * n_parts]
    load_sem, halo_send, halo_recv, pick_send, pick_recv, rs_send, rs_recv = rest[2 * n_parts:]
    rows, width = field.shape
    half = width // 2
    bs = raw_main.shape[1]
    kc = 6
    nb = rows // bs
    bw = 2 * bs
    me_d = lax.axis_index("depth")
    me_f = lax.axis_index("freq")
    first_row = me_d * rows

    for which, (src, dst) in enumerate(((main_hbm, raw_main), (side_hbm, raw_side))):
        def start(b, carry, src=src, dst=dst, which=which):
            at = pl.ds(pl.multiple_of(b * kc * bs, kc * bs), kc * bs)
            pltpu.make_async_copy(src.at[at], dst.at[at], load_sem.at[which, b]).start()
            return carry
        lax.fori_loop(0, nb, start, 0)

    barrier = pltpu.get_barrier_semaphore()
    for off in range(1, depth_n):
        pl.semaphore_signal(barrier, inc=1, device_id={"depth": lax.rem(me_d + off, depth_n)},
                            device_id_type=MESH)
    partners = []
    for j in range(bits):
        mine = lax.rem(me_f // (1 << j), 2)
        partners.append((mine, me_f + (1 - 2 * mine) * (1 << j)))
        pl.semaphore_signal(barrier, inc=1, device_id={"freq": partners[j][1]}, device_id_type=MESH)

    def put_w(parity, b, re, im):
        base = pl.multiple_of((b + 1) * bw, bw)
        top, low = pl.ds(base, bs), pl.ds(pl.multiple_of(base + bs, bs), bs)
        w_buf[parity, top, :half] = re
        w_buf[parity, top, half:] = im
        w_buf[parity, low, :half] = -im
        w_buf[parity, low, half:] = re

    from_col = lax.broadcasted_iota(jnp.int32, (width, width), 0)
    to_col = lax.broadcasted_iota(jnp.int32, (width, width), 1)
    wanted = jnp.where(to_col < half, 2 * to_col, 2 * (to_col - half) + 1)
    order = jnp.where(from_col == wanted, 1.0, 0.0).astype(BF16)

    def enter(b, carry):
        at = pl.ds(pl.multiple_of(b * bs, bs), bs)
        got = jnp.dot(field[at, :], order, preferred_element_type=F32).astype(BF16)
        put_w(0, b, got[:, :half], got[:, half:])
        return carry

    enter(0, 0)
    enter(nb - 1, 0)
    lax.fori_loop(1, nb - 1, enter, 0, unroll=2)
    zero_edge = jnp.zeros((bw, width), BF16)
    for parity in range(2):
        w_buf[parity, :bw, :] = zero_edge
        w_buf[parity, (nb + 1) * bw:, :] = zero_edge

    pl.semaphore_wait(barrier, depth_n - 1 + bits)

    def halo_copy(step, side):
        edge = (1 if side == 0 else nb) * bw
        to = lax.rem(me_d + (depth_n - 1 if side == 0 else 1), depth_n)
        return pltpu.make_async_remote_copy(
            src_ref=w_buf.at[step % 2, pl.ds(edge, bw)],
            dst_ref=halo.at[step, side],
            send_sem=halo_send.at[step, side],
            recv_sem=halo_recv.at[step, side],
            device_id={"depth": to},
            device_id_type=MESH,
        )

    has_above = me_d > 0
    has_below = me_d < depth_n - 1

    def halo_start(step):
        if depth_n == 1:
            return

        @pl.when(has_above)
        def _():
            halo_copy(step, 0).start()

        @pl.when(has_below)
        def _():
            halo_copy(step, 1).start()

    def halo_finish(step):
        if depth_n == 1:
            return

        @pl.when(has_above)
        def _():
            halo_copy(step, 0).wait_send()
            halo_copy(step, 1).wait_recv()
            w_buf[step % 2, :bw, :] = halo[step, 1]

        @pl.when(has_below)
        def _():
            halo_copy(step, 1).wait_send()
            halo_copy(step, 0).wait_recv()
            w_buf[step % 2, (nb + 1) * bw:, :] = halo[step, 0]

    halo_start(0)

    times = out.shape[1]
    lane = lax.broadcasted_iota(jnp.int32, (half, times), 1)

    def basis_of(c, carry):
        n = (c * times + lane).astype(F32)
        y = (freqs[...] * n) * F32(1.0 / NT)
        p = y - jnp.floor(y)
        r = jnp.where(p > 0.5, p - 1.0, p)
        z = r * r
        basis[c, :half, :] = poly(COS_TERMS, z).astype(BF16)
        basis[c, half:, :] = (-(r * poly(SIN_TERMS, z))).astype(BF16)
        return carry

    lax.fori_loop(0, freq_n, basis_of, 0)

    wr = weights[0:1, :]
    wi = weights[1:2, :]
    row_iota = lax.broadcasted_iota(jnp.int32, (bs, half), 0)

    def multiply(step, b):
        parity = step % 2
        near = pl.ds(pl.multiple_of(b * bw, bw), 3 * bw)
        acc = jnp.dot(ops[b], w_buf[parity, near, :], preferred_element_type=F32)
        m, c = acc[:bs], acc[bs:]
        re = m[:, :half] + wr * c[:, :half] - wi * c[:, half:]
        im = m[:, half:] + wr * c[:, half:] + wi * c[:, :half]
        damp = jnp.where(row_iota + (first_row + b * bs) >= floors[step], F32(0.5), F32(1.0))
        re = (damp * re).astype(BF16)
        im = (damp * im).astype(BF16)
        if step == STEPS - 1:
            at = pl.ds(pl.multiple_of(b * bs, bs), bs)
            final[at, :half] = re
            final[at, half:] = im
        else:
            put_w(1 - parity, b, re, im)

    def prepare(b):
        at = pl.ds(pl.multiple_of(b * kc * bs, kc * bs), kc * bs)
        for which, (src, dst) in enumerate(((main_hbm, raw_main), (side_hbm, raw_side))):
            pltpu.make_async_copy(src.at[at], dst.at[at], load_sem.at[which, b]).wait()
            spread[which] = dst[at, :].astype(F32)
            for piece in range(kc):
                ops[b, which * bs:(which + 1) * bs, piece * bs:(piece + 1) * bs] = spread[
                    which, pl.ds(piece, bs, stride=kc), :].astype(BF16)

    prepare(0)
    prepare(nb - 1)
    prepare(1)

    def first_step(b, carry):
        multiply(0, b)

        @pl.when(b + 1 < nb - 1)
        def _():
            prepare(b + 1)

        return carry

    lax.fori_loop(1, nb - 1, first_step, 0)
    halo_finish(0)
    multiply(0, 0)
    multiply(0, nb - 1)
    for step in range(1, STEPS):
        multiply(step, 1)
        multiply(step, 2)
        halo_start(step)

        def inner(b, carry, step=step):
            multiply(step, b)
            return carry

        lax.fori_loop(3, nb - 1, inner, 0, unroll=unroll_of(nb - 4))
        halo_finish(step)
        multiply(step, 0)
        multiply(step, nb - 1)

    here = out.shape[0]
    chunk = min(rows, 1024)

    def pick(owner):
        at = pl.ds(pl.multiple_of(owner * here, here), here)
        local = receivers[at, :] - first_row
        total = jnp.zeros((here, width), F32)
        for base in range(0, rows, chunk):
            marks = [
                jnp.where(local == lax.broadcasted_iota(jnp.int32, local.shape, 1) + (base + sub),
                          1.0, 0.0).astype(BF16)
                for sub in range(0, chunk, local.shape[1])
            ]
            total = total + jnp.dot(jnp.concatenate(marks, axis=1), final[base:base + chunk, :],
                                    preferred_element_type=F32)
        return total

    def pick_copy(off):
        return pltpu.make_async_remote_copy(
            src_ref=picked.at[off - 1],
            dst_ref=pick_in.at[off - 1],
            send_sem=pick_send.at[off - 1],
            recv_sem=pick_recv.at[off - 1],
            device_id={"depth": lax.rem(me_d + off, depth_n)},
            device_id_type=MESH,
        )

    for off in range(1, depth_n):
        picked[off - 1] = pick(lax.rem(me_d + off, depth_n)).astype(BF16)
    for off in range(1, depth_n):
        pick_copy(off).start()
    mine_rows = pick(me_d)
    for off in range(1, depth_n):
        pick_copy(off).wait()
        mine_rows = mine_rows + pick_in[off - 1].astype(F32)
    owned[...] = mine_rows.astype(BF16)

    def chunk_at(part_order, q):
        c = 0
        for t, j in enumerate(part_order):
            c = c + lax.rem(q // (1 << (bits - 1 - t)), 2) * (1 << j)
        return c

    def partial(part, q):
        start, count, part_order = plan[part]
        return jnp.dot(owned[start:start + count, :], basis[chunk_at(part_order, q)],
                       preferred_element_type=F32)

    def offset_of(stage):
        return freq_n - (freq_n >> stage)

    def rs_copy(part, stage):
        size = freq_n >> (stage + 1)
        at = pl.ds(offset_of(stage), size)
        j = plan[part][2][stage]
        return pltpu.make_async_remote_copy(
            src_ref=send_bufs[part].at[at],
            dst_ref=recv_bufs[part].at[at],
            send_sem=rs_send.at[part, stage],
            recv_sem=rs_recv.at[part, stage],
            device_id={"freq": partners[j][1]},
            device_id_type=MESH,
        )

    if bits == 0:
        out[...] = jnp.dot(owned[...], basis[0], preferred_element_type=F32) * factor
        return

    def sweep(size, body):
        def one(q, carry):
            body(q)
            return carry
        lax.fori_loop(0, size, one, 0, unroll=min(2, size))

    size = freq_n // 2
    for part in range(n_parts):
        mine = partners[plan[part][2][0]][0]

        def fill(q, part=part, mine=mine):
            send_bufs[part][q] = partial(part, (1 - mine) * size + q).astype(BF16)

        sweep(size, fill)
    for part in range(n_parts):
        rs_copy(part, 0).start()
    for part in range(n_parts):
        start, count, _ = plan[part]
        mine = partners[plan[part][2][0]][0]

        def keep(q, part=part, mine=mine, start=start, count=count):
            sums[q, start:start + count, :] = partial(part, mine * size + q)

        sweep(size, keep)
    for stage in range(bits):
        size = freq_n >> (stage + 1)
        base = offset_of(stage)
        last = stage == bits - 1
        for part in range(n_parts):
            start, count, part_order = plan[part]
            rs_copy(part, stage).wait()
            at = slice(start, start + count)
            if last:
                out[at, :] = (sums[0, at, :] + recv_bufs[part][base].astype(F32)) * factor
                continue
            nxt = size // 2
            mine = partners[part_order[stage + 1]][0]
            into = offset_of(stage + 1)

            def send(q, part=part, at=at, mine=mine, nxt=nxt, base=base, into=into):
                k = (1 - mine) * nxt + q
                send_bufs[part][into + q] = (
                    sums[k, at, :] + recv_bufs[part][base + k].astype(F32)).astype(BF16)

            sweep(nxt, send)
            rs_copy(part, stage + 1).start()

            def hold(q, part=part, at=at, mine=mine, nxt=nxt, base=base):
                k = mine * nxt + q
                sums[q, at, :] = sums[k, at, :] + recv_bufs[part][base + k].astype(F32)

            sweep(nxt, hold)


def local(depth_n, freq_n, pressure_field, block_main, block_coupled, coupling, frequencies,
          receivers, floors):
    rows, width = pressure_field.shape
    bs = block_main.shape[3]
    half = width // 2
    nb = rows // bs
    bits = freq_n.bit_length() - 1
    here = receivers.shape[0] // depth_n
    times = NT // freq_n
    factor = 1.0 / math.sqrt(frequencies.shape[0])
    plan = plan_of(here, bits)
    weights = coupling.reshape(half, 2).T
    own = lax.dynamic_slice_in_dim(frequencies, lax.axis_index("freq") * half, half)
    freqs = jnp.broadcast_to(own[:, None], (half, times))
    spots = jnp.broadcast_to(receivers[:, None], (receivers.shape[0], bs))
    vmem = pl.BlockSpec(memory_space=pltpu.VMEM)
    hbm = pl.BlockSpec(memory_space=pl.ANY)
    away = max(depth_n - 1, 1)
    slots = max(freq_n - 1, 1)
    return pl.pallas_call(
        functools.partial(kernel, depth_n, freq_n, bits, factor, plan),
        out_shape=jax.ShapeDtypeStruct((here, times), F32),
        in_specs=[vmem, hbm, hbm, vmem, vmem, vmem, pl.BlockSpec(memory_space=pltpu.SMEM)],
        out_specs=vmem,
        scratch_shapes=[
            pltpu.VMEM((rows * 6, bs), BF16),
            pltpu.VMEM((rows * 6, bs), BF16),
            pltpu.VMEM((2, 6 * bs, bs), F32),
            pltpu.VMEM((nb, 2 * bs, 6 * bs), BF16),
            pltpu.VMEM((2, (nb + 2) * 2 * bs, width), BF16),
            pltpu.VMEM((rows, width), BF16),
            pltpu.VMEM((STEPS, 2, 2 * bs, width), BF16),
            pltpu.VMEM((away, here, width), BF16),
            pltpu.VMEM((here, width), BF16),
            pltpu.VMEM((away, here, width), BF16),
            pltpu.VMEM((freq_n, width, times), BF16),
            pltpu.VMEM((max(freq_n // 2, 1), here, times), F32),
            *[pltpu.VMEM((slots, count, times), BF16) for _, count, _ in plan],
            *[pltpu.VMEM((slots, count, times), BF16) for _, count, _ in plan],
            pltpu.SemaphoreType.DMA((2, nb)),
            pltpu.SemaphoreType.DMA((STEPS, 2)),
            pltpu.SemaphoreType.DMA((STEPS, 2)),
            pltpu.SemaphoreType.DMA((away,)),
            pltpu.SemaphoreType.DMA((away,)),
            pltpu.SemaphoreType.DMA((len(plan), max(bits, 1))),
            pltpu.SemaphoreType.DMA((len(plan), max(bits, 1))),
        ],
        compiler_params=pltpu.CompilerParams(
            collective_id=0, has_side_effects=True, vmem_limit_bytes=64 * 1024 * 1024 - 128 * 1024
        ),
    )(
        pressure_field,
        block_main.reshape(rows * 6, bs),
        block_coupled.reshape(rows * 6, bs),
        weights,
        freqs,
        spots,
        floors,
    )


def solution(mesh):
    in_specs = (
        P("depth", "freq"),
        P("depth", None, None, None),
        P("depth", None, None, None),
        P("freq"),
        P(),
        P(),
        P(),
    )
    body = functools.partial(local, mesh.shape["depth"], mesh.shape["freq"])
    return jax.shard_map(body, mesh=mesh, in_specs=in_specs, out_specs=P("depth", "freq"),
                         check_vma=False)
```

profile of v0, /device:TPU:0, one launch (start us, length us, event | category | flops | bytes accessed | tf_op | source)
XLA Modules:
  0.0 80.7 jit_solution(9868295797870986959)
XLA Ops:
  0.0 0.8 dynamic_slice.3
  0.8 0.7 broadcast_in_dim.4.freqs
  1.5 0.8 %reshape.13 = f32[128,2]{1,0:T(8,128)S(1)} reshape(f32[256]{0:T(256)} %param.10) | data formatting | bytes 2048 | tf_op jit(solution)/shard_map/reshape | solution.py:370
  2.3 0.6 copy.8
  2.9 1.5 %broadcast_in_dim.5.receivers = s32[512,128]{1,0:T(8,128)} broadcast(s32[512]{0:T(512)} %param.12), dimensions={0} | broadcast | bytes 264192 | tf_op jit(solution)/shard_map/broadcast_in_dim | solution.py:373
  4.4 74.6 %shard_map.73 = f32[256,128]{1,0:T(8,128)} custom-call(bf16[4096,256]{1,0:T(8,128)(2,1)} %field.1, bf16[24576,128]{1,0:T(8,128)(2,1)} %bitcast.3, bf16[24576,128]{1,0:T(8,128)(2,1)} %bitcast.4, f32[2,128]{1,0:T(2,128)} %bitcast.5, f32[128,128]{1,0:T(8,128)} %broadcast_in_dim.4.freqs, s32[512,128]{1,0:T(8,128)} %broadcast_in_dim.5.receivers, s32[4]{0:T(128)} %floors.1), custom_call_target="tpu_custom_call" | custom-call | tf_op jit(solution)/shard_map/pallas_call | solution.py:378
  79.1 1.6 %copy.10 = f32[256,128]{1,0:T(8,128)} copy(f32[256,128]{1,0:T(8,128)} %shard_map.73) | data formatting | bytes 262144
where the time goes:
time: 80.9 us; the launch traced here: 80.7 us
  Pallas kernels  74.6 us (92%)
  local copies, waits for them, and re-layouts  6.01 us (7%)
    pallas_call x1, Pallas kernels, local(): pl.pallas_call(functools.partial(kernel, depth_n, freq_n, bits, factor, p...  74.6 us

commit v1 on v0

v1 whole, which is shorter than its diff:
```python
import functools
import math

import jax
import jax.numpy as jnp
from jax import lax
from jax.experimental import pallas as pl
from jax.experimental.pallas import tpu as pltpu
from jax.sharding import PartitionSpec as P

NT = 2048
STEPS = 4

COS_TERMS = (1.0, -19.739208221435547, 64.93939208984375, -85.45665740966797,
             60.242130279541016, -26.4046688079834, 7.800131320953369, -1.453112244606018)
SIN_TERMS = (6.2831854820251465, -41.34170150756836, 81.6052474975586, -76.70580291748047,
             42.05775451660156, -15.086565017700195, 3.7813189029693604, -0.6207787394523621)

MESH = pl.DeviceIdType.MESH
F32 = jnp.float32
BF16 = jnp.bfloat16
KC = 6
GROUP = 4


def poly(terms, z):
    total = jnp.full_like(z, terms[-1])
    for term in terms[-2::-1]:
        total = total * z + F32(term)
    return total


def kernel(depth_n, freq_n, near, factor, chunks,
           field, main_hbm, side_hbm, coupling, freqs, receivers, floors, out,
           fbuf, raw_main, raw_side, spread, ops, w_even, w_odd, final, halo, rows_f32, pick_out, pick_in,
           gathered, basis, kept, part_out, part_in,
           field_sem, load_sem, halo_send, halo_recv, pick_send, pick_recv, ag_send, ag_recv, rs_send, rs_recv):
    rows, width = fbuf.shape
    half = width // 2
    nb, _, bw, bs = ops.shape
    groups = nb // GROUP
    far = freq_n // near
    here, times = out.shape
    wide = NT // near
    me_d = lax.axis_index("depth")
    me_f = lax.axis_index("freq")
    me_near = lax.rem(me_f, near)
    me_far = me_f // near
    first_row = me_d * rows
    has_above = me_d > 0
    has_below = me_d < depth_n - 1
    w_bufs = (w_even, w_odd)

    field_copy = pltpu.make_async_copy(field, fbuf, field_sem)
    field_copy.start()
    span = GROUP * bs * KC

    def load_copy(which, grp):
        src, dst = ((main_hbm, raw_main), (side_hbm, raw_side))[which]
        at = pl.ds(grp * span, span)
        return pltpu.make_async_copy(src.at[at], dst.at[at], load_sem.at[which, grp])

    for grp in range(groups):
        for which in range(2):
            load_copy(which, grp).start()

    near_peers = []
    for off in range(1, near):
        peer = me_f
        for bit in range(near.bit_length() - 1):
            if off >> bit & 1:
                mine = lax.rem(me_f // (1 << bit), 2)
                peer = peer + (1 - 2 * mine) * (1 << bit)
        near_peers.append(peer)
    far_peers = [lax.rem(me_far + off, far) * near + me_near for off in range(1, far)]
    barrier = pltpu.get_barrier_semaphore()
    for off in range(1, depth_n):
        pl.semaphore_signal(barrier, inc=1, device_id={"depth": lax.rem(me_d + off, depth_n)},
                            device_id_type=MESH)
    for peer in near_peers + far_peers:
        pl.semaphore_signal(barrier, inc=1, device_id={"freq": peer}, device_id_type=MESH)

    lane = lax.broadcasted_iota(jnp.int32, (half, wide), 1)
    owner = lax.rem(lane // times + me_far, far)
    sample = ((owner * near + me_near) * times + lax.rem(lane, times)).astype(F32)
    for slot, peer in enumerate([me_f] + near_peers):
        row = freqs[pl.ds(peer, 1), :]
        column = jnp.broadcast_to(row, (half, half)).T
        for start in range(0, wide, half):
            n = sample[:, start:start + half]
            y = (column[:, :n.shape[1]] * n) * F32(1.0 / NT)
            p = y - jnp.floor(y)
            r = jnp.where(p > 0.5, p - 1.0, p)
            z = r * r
            basis[slot, :half, start:start + half] = poly(COS_TERMS, z).astype(BF16)
            basis[slot, half:, start:start + half] = (-(r * poly(SIN_TERMS, z))).astype(BF16)

    from_col = lax.broadcasted_iota(jnp.int32, (width, width), 0)
    to_col = lax.broadcasted_iota(jnp.int32, (width, width), 1)
    wanted = jnp.where(to_col < half, 2 * to_col, 2 * (to_col - half) + 1)
    order = jnp.where(from_col == wanted, 1.0, 0.0).astype(BF16)

    pairs = jnp.broadcast_to(jnp.concatenate([coupling[0:1, :], coupling[1:2, :]], axis=1), (16, width))
    weights = jnp.zeros((16, width), F32)
    rest = pairs
    for _ in range(3):
        piece = rest.astype(BF16)
        weights = weights + jnp.dot(piece, order, preferred_element_type=F32)
        rest = rest - piece.astype(F32)
    wr = weights[0:1, :half]
    wi = weights[0:1, half:]

    def put_w(dst, b, re, im):
        at = pl.ds(b * bs, bs)
        dst[0, at, :] = re
        dst[1, at, :] = im
        dst[2, at, :] = -im

    field_copy.wait()

    def enter(b):
        at = pl.ds(b * bs, bs)
        got = jnp.dot(fbuf[at, :], order, preferred_element_type=F32).astype(BF16)
        put_w(w_even, b, got[:, :half], got[:, half:])

    for b in [0, nb - 1] + list(range(1, nb - 1)):
        enter(b)

    blank = jnp.zeros(halo.shape[2:], BF16)

    @pl.when(jnp.logical_not(has_above))
    def _():
        for step in range(STEPS):
            halo[step, 0] = blank

    @pl.when(jnp.logical_not(has_below))
    def _():
        for step in range(STEPS):
            halo[step, 1] = blank

    final[:, rows:, :] = jnp.zeros((2, final.shape[1] - rows, half), F32)

    pl.semaphore_wait(barrier, depth_n - 1 + len(near_peers) + len(far_peers))

    def halo_copy(step, side):
        edge = 0 if side == 1 else nb - 1
        to = lax.rem(me_d + (depth_n - 1 if side == 1 else 1), depth_n)
        return pltpu.make_async_remote_copy(
            src_ref=w_bufs[step % 2].at[:, pl.ds(edge * bs, bs)],
            dst_ref=halo.at[step, side],
            send_sem=halo_send.at[step, side],
            recv_sem=halo_recv.at[step, side],
            device_id={"depth": to},
            device_id_type=MESH,
        )

    def halo_start(step):
        if depth_n == 1:
            return

        @pl.when(has_above)
        def _():
            halo_copy(step, 1).start()

        @pl.when(has_below)
        def _():
            halo_copy(step, 0).start()

    def halo_finish(step):
        if depth_n == 1:
            return

        @pl.when(has_above)
        def _():
            halo_copy(step, 1).wait_send()
            halo_copy(step, 0).wait_recv()

        @pl.when(has_below)
        def _():
            halo_copy(step, 0).wait_send()
            halo_copy(step, 1).wait_recv()

    halo_start(0)

    row_iota = lax.broadcasted_iota(jnp.int32, (bs, half), 0)

    def multiply(step, b):
        src = w_bufs[step % 2]
        pieces = []
        for k in range(3):
            at = b + k - 1
            if at < 0:
                re, im, neg = (halo[step, 0, c] for c in range(3))
            elif at >= nb:
                re, im, neg = (halo[step, 1, c] for c in range(3))
            else:
                re, im, neg = (src[c, pl.ds(at * bs, bs), :] for c in range(3))
            pieces.append(jnp.concatenate([re, im], axis=1))
            pieces.append(jnp.concatenate([neg, re], axis=1))
        rhs = jnp.concatenate(pieces, axis=0)
        lhs = jnp.concatenate([ops[b, piece] for piece in range(KC)], axis=1)
        acc = jnp.dot(lhs, rhs, preferred_element_type=F32)
        m, c = acc[:bs], acc[bs:]
        re = m[:, :half] + wr * c[:, :half] - wi * c[:, half:]
        im = m[:, half:] + wr * c[:, half:] + wi * c[:, :half]
        damp = jnp.where(row_iota + (first_row + b * bs) >= floors[step], F32(0.5), F32(1.0))
        re = damp * re
        im = damp * im
        if step == STEPS - 1:
            at = pl.ds(b * bs, bs)
            final[0, at, :] = re
            final[1, at, :] = im
        else:
            put_w(w_bufs[1 - step % 2], b, re.astype(BF16), im.astype(BF16))

    def prepare(b):
        at = pl.ds(b * KC * bs, KC * bs)
        for which, src in enumerate((raw_main, raw_side)):
            slot = (b % 2) * 2 + which
            spread[slot] = src[at, :].astype(F32)
            for piece in range(KC):
                ops[b, piece, which * bs:(which + 1) * bs, :] = spread[
                    slot, pl.ds(piece, bs, stride=KC), :].astype(BF16)

    for grp in range(groups):
        for which in range(2):
            load_copy(which, grp).wait()
        for i in range(GROUP):
            b = grp * GROUP + i
            prepare(b)
            before = b - GROUP
            if before > 0:
                multiply(0, before)
    halo_finish(0)
    multiply(0, 0)
    multiply(0, nb - 1)
    for b in range(nb - GROUP, nb - 1):
        multiply(0, b)
    halo_start(1)
    for step in range(1, STEPS):
        middle = nb // 2
        for b in range(1, middle):
            multiply(step, b)
        halo_finish(step)
        multiply(step, 0)
        multiply(step, nb - 1)
        for b in range(middle, nb - 1):
            multiply(step, b)
        if step + 1 < STEPS:
            halo_start(step + 1)

    def pick(owner):
        def one(j, carry):
            spot = receivers[owner * here + j] - first_row
            spot = jnp.where(jnp.logical_and(spot >= 0, spot < rows), spot, rows)
            for c in range(2):
                rows_f32[c, pl.ds(j, 1), :] = final[c, pl.ds(spot, 1), :]
            return carry
        lax.fori_loop(0, here, one, 0, unroll=16)

    def pick_copy(off):
        return pltpu.make_async_remote_copy(
            src_ref=pick_out.at[off - 1],
            dst_ref=pick_in.at[off - 1],
            send_sem=pick_send.at[off - 1],
            recv_sem=pick_recv.at[off - 1],
            device_id={"depth": lax.rem(me_d + off, depth_n)},
            device_id_type=MESH,
        )

    for off in range(1, depth_n):
        pick(lax.rem(me_d + off, depth_n))
        pick_out[off - 1] = rows_f32[...].astype(BF16)
        pick_copy(off).start()
    pick(me_d)
    for off in range(1, depth_n):
        pick_copy(off).wait()

    def ag_copy(off, chunk):
        start, count = chunks[chunk]
        at = pl.ds(start, count)
        return pltpu.make_async_remote_copy(
            src_ref=gathered.at[0, :, at],
            dst_ref=gathered.at[off, :, at],
            send_sem=ag_send.at[off - 1, chunk],
            recv_sem=ag_recv.at[off - 1, chunk],
            device_id={"freq": near_peers[off - 1]},
            device_id_type=MESH,
        )

    for chunk, (start, count) in enumerate(chunks):
        at = slice(start, start + count)
        mine = rows_f32[:, at, :]
        for off in range(1, depth_n):
            mine = mine + pick_in[off - 1, :, at, :].astype(F32)
        gathered[0, :, at, :] = mine.astype(BF16)
        for off in range(1, near):
            ag_copy(off, chunk).start()

    def rs_copy(off, chunk):
        start, count = chunks[chunk]
        at = pl.ds(start, count)
        return pltpu.make_async_remote_copy(
            src_ref=part_out.at[off - 1, at],
            dst_ref=part_in.at[off - 1, at],
            send_sem=rs_send.at[off - 1, chunk],
            recv_sem=rs_recv.at[off - 1, chunk],
            device_id={"freq": far_peers[off - 1]},
            device_id_type=MESH,
        )

    for chunk, (start, count) in enumerate(chunks):
        at = slice(start, start + count)
        for off in range(1, near):
            ag_copy(off, chunk).wait_recv()
        lhs = jnp.concatenate([gathered[slot, c, at, :] for slot in range(near) for c in range(2)], axis=1)
        rhs = jnp.concatenate([basis[slot] for slot in range(near)], axis=0)
        total = jnp.dot(lhs, rhs, preferred_element_type=F32)
        for off in range(1, far):
            part_out[off - 1, at, :] = total[:, off * times:(off + 1) * times].astype(BF16)
            rs_copy(off, chunk).start()
        kept[at, :] = total[:, :times]
    for chunk, (start, count) in enumerate(chunks):
        at = slice(start, start + count)
        total = kept[at, :]
        for off in range(1, far):
            rs_copy(off, chunk).wait_recv()
            total = total + part_in[off - 1, at, :].astype(F32)
        out[at, :] = total * factor
    for chunk in range(len(chunks)):
        for off in range(1, near):
            ag_copy(off, chunk).wait_send()
        for off in range(1, far):
            rs_copy(off, chunk).wait_send()


def local(depth_n, freq_n, pressure_field, block_main, block_coupled, coupling, frequencies,
          receivers, floors):
    rows, width = pressure_field.shape
    bs = block_main.shape[3]
    half = width // 2
    nb = rows // bs
    near = min(4, freq_n)
    far = freq_n // near
    here = receivers.shape[0] // depth_n
    times = NT // freq_n
    factor = 1.0 / math.sqrt(frequencies.shape[0])
    count = max(here // 4, 16)
    chunks = [(start, count) for start in range(0, here, count)]
    vmem = pl.BlockSpec(memory_space=pltpu.VMEM)
    hbm = pl.BlockSpec(memory_space=pl.ANY)
    smem = pl.BlockSpec(memory_space=pltpu.SMEM)
    away = max(depth_n - 1, 1)
    near_slots, far_slots = max(near - 1, 1), max(far - 1, 1)
    dma = pltpu.SemaphoreType.DMA
    return pl.pallas_call(
        functools.partial(kernel, depth_n, freq_n, near, factor, chunks),
        out_shape=jax.ShapeDtypeStruct((here, times), F32),
        in_specs=[hbm, hbm, hbm, vmem, vmem, smem, smem],
        out_specs=vmem,
        scratch_shapes=[
            pltpu.VMEM((rows, width), BF16),
            pltpu.VMEM((rows * KC, bs), BF16),
            pltpu.VMEM((rows * KC, bs), BF16),
            pltpu.VMEM((4, KC * bs, bs), F32),
            pltpu.VMEM((nb, KC, 2 * bs, bs), BF16),
            pltpu.VMEM((3, rows, half), BF16),
            pltpu.VMEM((3, rows, half), BF16),
            pltpu.VMEM((2, rows + 8, half), F32),
            pltpu.VMEM((STEPS, 2, 3, bs, half), BF16),
            pltpu.VMEM((2, here, half), F32),
            pltpu.VMEM((away, 2, here, half), BF16),
            pltpu.VMEM((away, 2, here, half), BF16),
            pltpu.VMEM((near, 2, here, half), BF16),
            pltpu.VMEM((near, width, NT // near), BF16),
            pltpu.VMEM((here, times), F32),
            pltpu.VMEM((far_slots, here, times), BF16),
            pltpu.VMEM((far_slots, here, times), BF16),
            dma(()),
            dma((2, nb // GROUP)),
            dma((STEPS, 2)),
            dma((STEPS, 2)),
            dma((away,)),
            dma((away,)),
            dma((near_slots, len(chunks))),
            dma((near_slots, len(chunks))),
            dma((far_slots, len(chunks))),
            dma((far_slots, len(chunks))),
        ],
        compiler_params=pltpu.CompilerParams(
            collective_id=0, has_side_effects=True, vmem_limit_bytes=64 * 1024 * 1024 - 128 * 1024
        ),
    )(
        pressure_field,
        block_main.reshape(rows * KC, bs),
        block_coupled.reshape(rows * KC, bs),
        coupling.reshape(2, half),
        frequencies.reshape(freq_n, half),
        receivers,
        floors,
    )


def solution(mesh):
    in_specs = (
        P("depth", "freq"),
        P("depth", None, None, None),
        P("depth", None, None, None),
        P("freq"),
        P(),
        P(),
        P(),
    )
    body = functools.partial(local, mesh.shape["depth"], mesh.shape["freq"])
    return jax.shard_map(body, mesh=mesh, in_specs=in_specs, out_specs=P("depth", "freq"),
                         check_vma=False)
```

time: 80.9 us -> 48 us (0.59)
  Pallas kernels: 74.6 us -> 46.2 us
  local copies, waits for them, and re-layouts: 6.01 us -> 1.57 us
    pallas_call x1, Pallas kernels: 74.6 us -> 46.2 us  [local(): pl.pallas_call(functools.partial(kernel, depth_n, freq_n, near, factor, c...]
    broadcast_in_dim x2 -> x0, local copies, waits for them, and re-layouts: 2.22 us -> none  [the longest x1 1.51 us: local(): spots = jnp.broadcast_to(receivers[:, None], (receivers.shape[0], bs))]
    reshape x2 -> x0, local copies, waits for them, and re-layouts: 1.46 us -> none  [local(): weights = coupling.reshape(half, 2).T]
where the time goes in v1:
time: 48 us; the launch traced here: 47.8 us
  Pallas kernels  46.2 us (96%)
  local copies, waits for them, and re-layouts  1.57 us (3%)
    pallas_call x1, Pallas kernels, local(): pl.pallas_call(functools.partial(kernel, depth_n, freq_n, near, factor, c...  46.2 us
    unnamed x1, local copies, waits for them, and re-layouts  1.57 us

profile of v1, /device:TPU:0, one launch (start us, length us, event | category | flops | bytes accessed | tf_op | source)
XLA Modules:
  0.0 47.8 jit_solution(12534968492409037466)
XLA Ops:
  0.0 46.2 %shard_map.73 = f32[256,128]{1,0:T(8,128)} custom-call(bf16[4096,256]{1,0:T(8,128)(2,1)} %field.1, bf16[24576,128]{1,0:T(8,128)(2,1)} %bitcast.4, bf16[24576,128]{1,0:T(8,128)(2,1)} %bitcast.5, f32[2,128]{1,0:T(2,128)} %bitcast.7, f32[16,128]{1,0:T(8,128)} %bitcast.6, s32[512]{0:T(512)} %receivers.1, s32[4]{0:T(128)} %floors.1), custom_call_target="tpu_custom_call" | custom-call | tf_op jit(solution)/shard_map/pallas_call | solution.py:356
  46.3 1.6 %copy.9 = f32[256,128]{1,0:T(8,128)} copy(f32[256,128]{1,0:T(8,128)} %shard_map.73) | data formatting | bytes 262144

commit v2 on v1

--- a/solution.py
+++ b/solution.py
@@ -20,7 +20,11 @@
 F32 = jnp.float32
 BF16 = jnp.bfloat16
 KC = 6
-GROUP = 4
+VMEM_LIMIT = 46 * 1024 * 1024
+GROUPS = (4, 4, 4, 4, 4, 4, 4, 4)
+MEET = 4
+AHEAD = 5
+FIELD_PARTS = 4
 
 
 def poly(terms, z):
@@ -30,15 +34,22 @@
     return total
 
 
+def group_cuts(nb):
+    cuts = [0]
+    while cuts[-1] < nb:
+        cuts.append(min(nb, cuts[-1] + GROUPS[min(len(cuts) - 1, len(GROUPS) - 1)]))
+    return cuts
+
+
 def kernel(depth_n, freq_n, near, factor, chunks,
            field, main_hbm, side_hbm, coupling, freqs, receivers, floors, out,
-           fbuf, raw_main, raw_side, spread, ops, w_even, w_odd, final, halo, rows_f32, pick_out, pick_in,
+           fbuf, raw_main, raw_side, ops, w_even, w_odd, final, halo, rows_f32, pick_out, pick_in,
            gathered, basis, kept, part_out, part_in,
            field_sem, load_sem, halo_send, halo_recv, pick_send, pick_recv, ag_send, ag_recv, rs_send, rs_recv):
     rows, width = fbuf.shape
     half = width // 2
     nb, _, bw, bs = ops.shape
-    groups = nb // GROUP
+    cuts = group_cuts(nb)
     far = freq_n // near
     here, times = out.shape
     wide = NT // near
@@ -51,18 +62,24 @@
     has_below = me_d < depth_n - 1
     w_bufs = (w_even, w_odd)
 
-    field_copy = pltpu.make_async_copy(field, fbuf, field_sem)
-    field_copy.start()
-    span = GROUP * bs * KC
+    def field_copy(part):
+        at = pl.ds(part * (rows // FIELD_PARTS), rows // FIELD_PARTS)
+        return pltpu.make_async_copy(field.at[at], fbuf.at[at], field_sem.at[part])
+
+    for part in range(FIELD_PARTS):
+        field_copy(part).start()
+
+    def load_start(grp):
+        if grp < len(cuts) - 1:
+            for which in range(2):
+                load_copy(which, grp).start()
 
     def load_copy(which, grp):
         src, dst = ((main_hbm, raw_main), (side_hbm, raw_side))[which]
-        at = pl.ds(grp * span, span)
+        at = pl.ds(cuts[grp] * bs * KC, (cuts[grp + 1] - cuts[grp]) * bs * KC)
         return pltpu.make_async_copy(src.at[at], dst.at[at], load_sem.at[which, grp])
 
-    for grp in range(groups):
-        for which in range(2):
-            load_copy(which, grp).start()
+    load_start(0)
 
     near_peers = []
     for off in range(1, near):
@@ -95,6 +112,9 @@
             basis[slot, :half, start:start + half] = poly(COS_TERMS, z).astype(BF16)
             basis[slot, half:, start:start + half] = (-(r * poly(SIN_TERMS, z))).astype(BF16)
 
+    for grp in range(1, AHEAD):
+        load_start(grp)
+
     from_col = lax.broadcasted_iota(jnp.int32, (width, width), 0)
     to_col = lax.broadcasted_iota(jnp.int32, (width, width), 1)
     wanted = jnp.where(to_col < half, 2 * to_col, 2 * (to_col - half) + 1)
@@ -116,7 +136,8 @@
         dst[1, at, :] = im
         dst[2, at, :] = -im
 
-    field_copy.wait()
+    for part in range(FIELD_PARTS):
+        field_copy(part).wait()
 
     def enter(b):
         at = pl.ds(b * bs, bs)
@@ -139,8 +160,6 @@
             halo[step, 1] = blank
 
     final[:, rows:, :] = jnp.zeros((2, final.shape[1] - rows, half), F32)
-
-    pl.semaphore_wait(barrier, depth_n - 1 + len(near_peers) + len(far_peers))
 
     def halo_copy(step, side):
         edge = 0 if side == 1 else nb - 1
@@ -179,8 +198,6 @@
         def _():
             halo_copy(step, 0).wait_send()
             halo_copy(step, 1).wait_recv()
-
-    halo_start(0)
 
     row_iota = lax.broadcasted_iota(jnp.int32, (bs, half), 0)
 
@@ -198,7 +215,15 @@
             pieces.append(jnp.concatenate([re, im], axis=1))
             pieces.append(jnp.concatenate([neg, re], axis=1))
         rhs = jnp.concatenate(pieces, axis=0)
-        lhs = jnp.concatenate([ops[b, piece] for piece in range(KC)], axis=1)
+        if step == 0:
+            lhs = jnp.concatenate([
+                jnp.concatenate([raw[pl.ds(b * KC * bs + piece, bs, stride=KC), :] for piece in range(KC)], axis=1)
+                for raw in (raw_main, raw_side)
+            ], axis=0)
+            for piece in range(KC):
+                ops[b, piece] = lhs[:, piece * bs:(piece + 1) * bs]
+        else:
+            lhs = jnp.concatenate([ops[b, piece] for piece in range(KC)], axis=1)
         acc = jnp.dot(lhs, rhs, preferred_element_type=F32)
         m, c = acc[:bs], acc[bs:]
         re = m[:, :half] + wr * c[:, :half] - wi * c[:, half:]
@@ -213,29 +238,19 @@
         else:
             put_w(w_bufs[1 - step % 2], b, re.astype(BF16), im.astype(BF16))
 
-    def prepare(b):
-        at = pl.ds(b * KC * bs, KC * bs)
-        for which, src in enumerate((raw_main, raw_side)):
-            slot = (b % 2) * 2 + which
-            spread[slot] = src[at, :].astype(F32)
-            for piece in range(KC):
-                ops[b, piece, which * bs:(which + 1) * bs, :] = spread[
-                    slot, pl.ds(piece, bs, stride=KC), :].astype(BF16)
-
-    for grp in range(groups):
+    for grp in range(len(cuts) - 1):
         for which in range(2):
             load_copy(which, grp).wait()
-        for i in range(GROUP):
-            b = grp * GROUP + i
-            prepare(b)
-            before = b - GROUP
-            if before > 0:
-                multiply(0, before)
-    halo_finish(0)
-    multiply(0, 0)
-    multiply(0, nb - 1)
-    for b in range(nb - GROUP, nb - 1):
-        multiply(0, b)
+        load_start(grp + AHEAD)
+        if grp == MEET:
+            pl.semaphore_wait(barrier, depth_n - 1 + len(near_peers) + len(far_peers))
+            halo_start(0)
+        if cuts[grp + 1] == nb:
+            halo_finish(0)
+            multiply(0, 0)
+            multiply(0, nb - 1)
+        for b in range(max(cuts[grp], 1), min(cuts[grp + 1], nb - 1)):
+            multiply(0, b)
     halo_start(1)
     for step in range(1, STEPS):
         middle = nb // 2
@@ -249,39 +264,41 @@
         if step + 1 < STEPS:
             halo_start(step + 1)
 
-    def pick(owner):
+    limit = jnp.uint32(rows)
+
+    def pick(owner, dst, chunk):
+        start, count = chunks[chunk]
+
         def one(j, carry):
-            spot = receivers[owner * here + j] - first_row
-            spot = jnp.where(jnp.logical_and(spot >= 0, spot < rows), spot, rows)
+            spot = receivers[owner * here + start + j] - first_row
+            spot = jnp.minimum(spot.astype(jnp.uint32), limit).astype(jnp.int32)
             for c in range(2):
-                rows_f32[c, pl.ds(j, 1), :] = final[c, pl.ds(spot, 1), :]
+                dst[c, pl.ds(start + j, 1), :] = final[c, pl.ds(spot, 1), :]
             return carry
-        lax.fori_loop(0, here, one, 0, unroll=16)
-
-    def pick_copy(off):
+        lax.fori_loop(0, count, one, 0, unroll=16)
+
+    def pick_copy(off, chunk):
         return pltpu.make_async_remote_copy(
-            src_ref=pick_out.at[off - 1],
-            dst_ref=pick_in.at[off - 1],
-            send_sem=pick_send.at[off - 1],
-            recv_sem=pick_recv.at[off - 1],
+            src_ref=pick_out.at[off - 1, chunk],
+            dst_ref=pick_in.at[off - 1, chunk],
+            send_sem=pick_send.at[off - 1, chunk],
+            recv_sem=pick_recv.at[off - 1, chunk],
             device_id={"depth": lax.rem(me_d + off, depth_n)},
             device_id_type=MESH,
         )
 
     for off in range(1, depth_n):
-        pick(lax.rem(me_d + off, depth_n))
-        pick_out[off - 1] = rows_f32[...].astype(BF16)
-        pick_copy(off).start()
-    pick(me_d)
-    for off in range(1, depth_n):
-        pick_copy(off).wait()
+        for chunk, (start, count) in enumerate(chunks):
+            pick(lax.rem(me_d + off, depth_n), rows_f32.at[off], chunk)
+            pick_out[off - 1, chunk] = rows_f32[off, :, start:start + count, :].astype(BF16)
+            pick_copy(off, chunk).start()
+    for chunk in range(len(chunks)):
+        pick(me_d, rows_f32.at[0], chunk)
 
     def ag_copy(off, chunk):
-        start, count = chunks[chunk]
-        at = pl.ds(start, count)
         return pltpu.make_async_remote_copy(
-            src_ref=gathered.at[0, :, at],
-            dst_ref=gathered.at[off, :, at],
+            src_ref=gathered.at[0, chunk],
+            dst_ref=gathered.at[off, chunk],
             send_sem=ag_send.at[off - 1, chunk],
             recv_sem=ag_recv.at[off - 1, chunk],
             device_id={"freq": near_peers[off - 1]},
@@ -290,10 +307,11 @@
 
     for chunk, (start, count) in enumerate(chunks):
         at = slice(start, start + count)
-        mine = rows_f32[:, at, :]
+        mine = rows_f32[0, :, at, :]
         for off in range(1, depth_n):
-            mine = mine + pick_in[off - 1, :, at, :].astype(F32)
-        gathered[0, :, at, :] = mine.astype(BF16)
+            pick_copy(off, chunk).wait()
+            mine = mine + pick_in[off - 1, chunk].astype(F32)
+        gathered[0, chunk] = mine.astype(BF16)
         for off in range(1, near):
             ag_copy(off, chunk).start()
 
@@ -313,7 +331,7 @@
         at = slice(start, start + count)
         for off in range(1, near):
             ag_copy(off, chunk).wait_recv()
-        lhs = jnp.concatenate([gathered[slot, c, at, :] for slot in range(near) for c in range(2)], axis=1)
+        lhs = jnp.concatenate([gathered[slot, chunk, c] for slot in range(near) for c in range(2)], axis=1)
         rhs = jnp.concatenate([basis[slot] for slot in range(near)], axis=0)
         total = jnp.dot(lhs, rhs, preferred_element_type=F32)
         for off in range(1, far):
@@ -348,7 +366,7 @@
     count = max(here // 4, 16)
     chunks = [(start, count) for start in range(0, here, count)]
     vmem = pl.BlockSpec(memory_space=pltpu.VMEM)
-    hbm = pl.BlockSpec(memory_space=pl.ANY)
+    hbm = pl.BlockSpec(memory_space=pltpu.HBM)
     smem = pl.BlockSpec(memory_space=pltpu.SMEM)
     away = max(depth_n - 1, 1)
     near_slots, far_slots = max(near - 1, 1), max(far - 1, 1)
@@ -362,35 +380,34 @@
             pltpu.VMEM((rows, width), BF16),
             pltpu.VMEM((rows * KC, bs), BF16),
             pltpu.VMEM((rows * KC, bs), BF16),
-            pltpu.VMEM((4, KC * bs, bs), F32),
             pltpu.VMEM((nb, KC, 2 * bs, bs), BF16),
             pltpu.VMEM((3, rows, half), BF16),
             pltpu.VMEM((3, rows, half), BF16),
             pltpu.VMEM((2, rows + 8, half), F32),
             pltpu.VMEM((STEPS, 2, 3, bs, half), BF16),
-            pltpu.VMEM((2, here, half), F32),
-            pltpu.VMEM((away, 2, here, half), BF16),
-            pltpu.VMEM((away, 2, here, half), BF16),
-            pltpu.VMEM((near, 2, here, half), BF16),
+            pltpu.VMEM((depth_n, 2, here, half), F32),
+            pltpu.VMEM((away, len(chunks), 2, count, half), BF16),
+            pltpu.VMEM((away, len(chunks), 2, count, half), BF16),
+            pltpu.VMEM((near, len(chunks), 2, count, half), BF16),
             pltpu.VMEM((near, width, NT // near), BF16),
             pltpu.VMEM((here, times), F32),
             pltpu.VMEM((far_slots, here, times), BF16),
             pltpu.VMEM((far_slots, here, times), BF16),
-            dma(()),
-            dma((2, nb // GROUP)),
+            dma((FIELD_PARTS,)),
+            dma((2, len(group_cuts(nb)) - 1)),
             dma((STEPS, 2)),
             dma((STEPS, 2)),
-            dma((away,)),
-            dma((away,)),
+            dma((away, len(chunks))),
+            dma((away, len(chunks))),
             dma((near_slots, len(chunks))),
             dma((near_slots, len(chunks))),
             dma((far_slots, len(chunks))),
             dma((far_slots, len(chunks))),
         ],
         compiler_params=pltpu.CompilerParams(
-            collective_id=0, has_side_effects=True, vmem_limit_bytes=64 * 1024 * 1024 - 128 * 1024
+            collective_id=0, has_side_effects=True, vmem_limit_bytes=VMEM_LIMIT
         ),
-    )(
+    )(*(pltpu.with_memory_space_constraint(x, pltpu.HBM) for x in (
         pressure_field,
         block_main.reshape(rows * KC, bs),
         block_coupled.reshape(rows * KC, bs),
@@ -398,7 +415,7 @@
         frequencies.reshape(freq_n, half),
         receivers,
         floors,
-    )
+    )))
 
 
 def solution(mesh):

time: 48 us -> 39.7 us (0.83)
  Pallas kernels: 46.2 us -> 38.9 us
  local copies, waits for them, and re-layouts: 1.57 us -> 0.66 us
    pallas_call x1, Pallas kernels: 46.2 us -> 38.9 us  [local(): pl.pallas_call(functools.partial(kernel, depth_n, freq_n, near, factor, c...]
    unnamed x1, local copies, waits for them, and re-layouts: 1.57 us -> 0.66 us
where the time goes in v2:
time: 39.7 us; the launch traced here: 39.6 us
  Pallas kernels  38.9 us (98%)
  local copies, waits for them, and re-layouts  0.66 us (2%)
    pallas_call x1, Pallas kernels, local(): pl.pallas_call(functools.partial(kernel, depth_n, freq_n, near, factor, c...  38.9 us

profile of v2, /device:TPU:0, one launch (start us, length us, event | category | flops | bytes accessed | tf_op | source)
XLA Modules:
  0.0 39.6 jit_solution(4028435468475606728)
XLA Ops:
  0.0 38.9 %shard_map.73 = f32[256,128]{1,0:T(8,128)S(1)} custom-call(bf16[4096,256]{1,0:T(8,128)(2,1)} %field.1, bf16[24576,128]{1,0:T(8,128)(2,1)} %bitcast.4, bf16[24576,128]{1,0:T(8,128)(2,1)} %bitcast.5, f32[2,128]{1,0:T(2,128)} %bitcast.7, f32[16,128]{1,0:T(8,128)} %bitcast.6, s32[512]{0:T(512)} %receivers.1, s32[4]{0:T(128)} %floors.1), custom_call_target="tpu_custom_call" | custom-call | tf_op jit(solution)/shard_map/pallas_call | solution.py:374
  38.9 0.7 %copy.9 = f32[256,128]{1,0:T(8,128)} copy(f32[256,128]{1,0:T(8,128)S(1)} %shard_map.73) | data formatting | bytes 262144

commit v3 on v2

--- a/solution.py
+++ b/solution.py
@@ -21,10 +21,11 @@
 BF16 = jnp.bfloat16
 KC = 6
 VMEM_LIMIT = 46 * 1024 * 1024
-GROUPS = (4, 4, 4, 4, 4, 4, 4, 4)
-MEET = 4
-AHEAD = 5
-FIELD_PARTS = 4
+GROUPS = (4, 8, 8, 8, 4)
+MEET = 3
+CHUNKS = ((0, 5), (5, 5), (10, 4), (14, 2))
+AHEAD = 3
+FIELD_PARTS = 8
 
 
 def poly(terms, z):
@@ -42,10 +43,10 @@
 
 
 def kernel(depth_n, freq_n, near, factor, chunks,
-           field, main_hbm, side_hbm, coupling, freqs, receivers, floors, out,
-           fbuf, raw_main, raw_side, ops, w_even, w_odd, final, halo, rows_f32, pick_out, pick_in,
+           field, main_hbm, side_hbm, coupling_hbm, freqs_hbm, receivers_hbm, floors_hbm, out,
+           coupling, freqs, receivers, floors, fbuf, raw_main, raw_side, ops, w_even, w_odd, final, halo, rows_f32, pick_out, pick_in,
            gathered, basis, kept, part_out, part_in,
-           field_sem, load_sem, halo_send, halo_recv, pick_send, pick_recv, ag_send, ag_recv, rs_send, rs_recv):
+           small_sem, field_sem, load_sem, halo_send, halo_recv, pick_send, pick_recv, ag_send, ag_recv, rs_send, rs_recv):
     rows, width = fbuf.shape
     half = width // 2
     nb, _, bw, bs = ops.shape
@@ -64,7 +65,7 @@
 
     def field_copy(part):
         at = pl.ds(part * (rows // FIELD_PARTS), rows // FIELD_PARTS)
-        return pltpu.make_async_copy(field.at[at], fbuf.at[at], field_sem.at[part])
+        return pltpu.make_async_copy(field.at[at], fbuf.at[at], field_sem)
 
     for part in range(FIELD_PARTS):
         field_copy(part).start()
@@ -79,6 +80,13 @@
         at = pl.ds(cuts[grp] * bs * KC, (cuts[grp + 1] - cuts[grp]) * bs * KC)
         return pltpu.make_async_copy(src.at[at], dst.at[at], load_sem.at[which, grp])
 
+    smalls = [
+        pltpu.make_async_copy(src, dst, small_sem.at[i])
+        for i, (src, dst) in enumerate(((coupling_hbm, coupling), (floors_hbm, floors),
+                                        (freqs_hbm, freqs), (receivers_hbm, receivers)))
+    ]
+    for copy in smalls:
+        copy.start()
     load_start(0)
 
     near_peers = []
@@ -97,29 +105,14 @@
     for peer in near_peers + far_peers:
         pl.semaphore_signal(barrier, inc=1, device_id={"freq": peer}, device_id_type=MESH)
 
-    lane = lax.broadcasted_iota(jnp.int32, (half, wide), 1)
-    owner = lax.rem(lane // times + me_far, far)
-    sample = ((owner * near + me_near) * times + lax.rem(lane, times)).astype(F32)
-    for slot, peer in enumerate([me_f] + near_peers):
-        row = freqs[pl.ds(peer, 1), :]
-        column = jnp.broadcast_to(row, (half, half)).T
-        for start in range(0, wide, half):
-            n = sample[:, start:start + half]
-            y = (column[:, :n.shape[1]] * n) * F32(1.0 / NT)
-            p = y - jnp.floor(y)
-            r = jnp.where(p > 0.5, p - 1.0, p)
-            z = r * r
-            basis[slot, :half, start:start + half] = poly(COS_TERMS, z).astype(BF16)
-            basis[slot, half:, start:start + half] = (-(r * poly(SIN_TERMS, z))).astype(BF16)
-
-    for grp in range(1, AHEAD):
-        load_start(grp)
+    load_start(1)
 
     from_col = lax.broadcasted_iota(jnp.int32, (width, width), 0)
     to_col = lax.broadcasted_iota(jnp.int32, (width, width), 1)
     wanted = jnp.where(to_col < half, 2 * to_col, 2 * (to_col - half) + 1)
     order = jnp.where(from_col == wanted, 1.0, 0.0).astype(BF16)
 
+    smalls[0].wait()
     pairs = jnp.broadcast_to(jnp.concatenate([coupling[0:1, :], coupling[1:2, :]], axis=1), (16, width))
     weights = jnp.zeros((16, width), F32)
     rest = pairs
@@ -136,8 +129,24 @@
         dst[1, at, :] = im
         dst[2, at, :] = -im
 
-    for part in range(FIELD_PARTS):
-        field_copy(part).wait()
+    blank = jnp.zeros(halo.shape[2:], BF16)
+
+    @pl.when(jnp.logical_not(has_above))
+    def _():
+        for step in range(STEPS):
+            halo[step, 0] = blank
+
+    @pl.when(jnp.logical_not(has_below))
+    def _():
+        for step in range(STEPS):
+            halo[step, 1] = blank
+
+    final[:, rows:, :] = jnp.zeros((2, final.shape[1] - rows, half), F32)
+
+    for copy in smalls[1:]:
+        copy.wait()
+    pltpu.make_async_copy(field, fbuf, field_sem).wait()
+    load_start(AHEAD - 1)
 
     def enter(b):
         at = pl.ds(b * bs, bs)
@@ -147,28 +156,14 @@
     for b in [0, nb - 1] + list(range(1, nb - 1)):
         enter(b)
 
-    blank = jnp.zeros(halo.shape[2:], BF16)
-
-    @pl.when(jnp.logical_not(has_above))
-    def _():
-        for step in range(STEPS):
-            halo[step, 0] = blank
-
-    @pl.when(jnp.logical_not(has_below))
-    def _():
-        for step in range(STEPS):
-            halo[step, 1] = blank
-
-    final[:, rows:, :] = jnp.zeros((2, final.shape[1] - rows, half), F32)
-
     def halo_copy(step, side):
         edge = 0 if side == 1 else nb - 1
         to = lax.rem(me_d + (depth_n - 1 if side == 1 else 1), depth_n)
         return pltpu.make_async_remote_copy(
             src_ref=w_bufs[step % 2].at[:, pl.ds(edge * bs, bs)],
             dst_ref=halo.at[step, side],
-            send_sem=halo_send.at[step, side],
-            recv_sem=halo_recv.at[step, side],
+            send_sem=halo_send.at[step % 2, side],
+            recv_sem=halo_recv.at[step % 2, side],
             device_id={"depth": to},
             device_id_type=MESH,
         )
@@ -277,11 +272,11 @@
             return carry
         lax.fori_loop(0, count, one, 0, unroll=16)
 
-    def pick_copy(off, chunk):
-        return pltpu.make_async_remote_copy(
-            src_ref=pick_out.at[off - 1, chunk],
-            dst_ref=pick_in.at[off - 1, chunk],
-            send_sem=pick_send.at[off - 1, chunk],
+    def pick_copy(off, at, chunk):
+        return pltpu.make_async_remote_copy(
+            src_ref=pick_out.at[off - 1, :, at],
+            dst_ref=pick_in.at[off - 1, :, at],
+            send_sem=pick_send.at[off - 1],
             recv_sem=pick_recv.at[off - 1, chunk],
             device_id={"depth": lax.rem(me_d + off, depth_n)},
             device_id_type=MESH,
@@ -290,18 +285,29 @@
     for off in range(1, depth_n):
         for chunk, (start, count) in enumerate(chunks):
             pick(lax.rem(me_d + off, depth_n), rows_f32.at[off], chunk)
-            pick_out[off - 1, chunk] = rows_f32[off, :, start:start + count, :].astype(BF16)
-            pick_copy(off, chunk).start()
+            pick_out[off - 1, :, start:start + count, :] = rows_f32[off, :, start:start + count, :].astype(BF16)
+            pick_copy(off, pl.ds(start, count), chunk).start()
     for chunk in range(len(chunks)):
         pick(me_d, rows_f32.at[0], chunk)
 
-    def ag_copy(off, chunk):
-        return pltpu.make_async_remote_copy(
-            src_ref=gathered.at[0, chunk],
-            dst_ref=gathered.at[off, chunk],
-            send_sem=ag_send.at[off - 1, chunk],
-            recv_sem=ag_recv.at[off - 1, chunk],
+    def ag_copy(off, at, chunk):
+        return pltpu.make_async_remote_copy(
+            src_ref=gathered.at[0, :, at],
+            dst_ref=gathered.at[off, :, at],
+            send_sem=ag_send,
+            recv_sem=ag_recv.at[chunk],
             device_id={"freq": near_peers[off - 1]},
+            device_id_type=MESH,
+        )
+
+    def ag_all(at, chunk):
+        others = gathered.at[pl.ds(1, near - 1), :, at]
+        return pltpu.make_async_remote_copy(
+            src_ref=others,
+            dst_ref=others,
+            send_sem=ag_send,
+            recv_sem=ag_recv.at[chunk],
+            device_id={"freq": near_peers[0]},
             device_id_type=MESH,
         )
 
@@ -309,47 +315,73 @@
         at = slice(start, start + count)
         mine = rows_f32[0, :, at, :]
         for off in range(1, depth_n):
-            pick_copy(off, chunk).wait()
-            mine = mine + pick_in[off - 1, chunk].astype(F32)
-        gathered[0, chunk] = mine.astype(BF16)
-        for off in range(1, near):
-            ag_copy(off, chunk).start()
-
-    def rs_copy(off, chunk):
-        start, count = chunks[chunk]
-        at = pl.ds(start, count)
+            pick_copy(off, pl.ds(start, count), chunk).wait_recv()
+            mine = mine + pick_in[off - 1, :, at, :].astype(F32)
+        gathered[0, :, at, :] = mine.astype(BF16)
+        for off in range(near - 1, 0, -1):
+            ag_copy(off, pl.ds(start, count), chunk).start()
+
+    lane = lax.broadcasted_iota(jnp.int32, (half, wide), 1)
+    owner = lax.rem(lane // times + me_far, far)
+    sample = ((owner * near + me_near) * times + lax.rem(lane, times)).astype(F32)
+    for slot, peer in enumerate([me_f] + near_peers):
+        row = freqs[pl.ds(peer, 1), :]
+        column = jnp.broadcast_to(row, (half, half)).T
+        for start in range(0, wide, half):
+            n = sample[:, start:start + half]
+            y = (column[:, :n.shape[1]] * n) * F32(1.0 / NT)
+            p = y - jnp.floor(y)
+            r = jnp.where(p > 0.5, p - 1.0, p)
+            z = r * r
+            basis[slot, :half, start:start + half] = poly(COS_TERMS, z).astype(BF16)
+            basis[slot, half:, start:start + half] = (-(r * poly(SIN_TERMS, z))).astype(BF16)
+
+    def rs_copy(off, at, chunk):
         return pltpu.make_async_remote_copy(
             src_ref=part_out.at[off - 1, at],
             dst_ref=part_in.at[off - 1, at],
-            send_sem=rs_send.at[off - 1, chunk],
-            recv_sem=rs_recv.at[off - 1, chunk],
+            send_sem=rs_send,
+            recv_sem=rs_recv.at[chunk],
             device_id={"freq": far_peers[off - 1]},
+            device_id_type=MESH,
+        )
+
+    def rs_all(at, chunk):
+        return pltpu.make_async_remote_copy(
+            src_ref=part_out.at[:, at],
+            dst_ref=part_in.at[:, at],
+            send_sem=rs_send,
+            recv_sem=rs_recv.at[chunk],
+            device_id={"freq": far_peers[0]},
             device_id_type=MESH,
         )
 
     for chunk, (start, count) in enumerate(chunks):
         at = slice(start, start + count)
-        for off in range(1, near):
-            ag_copy(off, chunk).wait_recv()
-        lhs = jnp.concatenate([gathered[slot, chunk, c] for slot in range(near) for c in range(2)], axis=1)
+        if near > 1:
+            ag_all(pl.ds(start, count), chunk).wait_recv()
+        lhs = jnp.concatenate([gathered[slot, c, at, :] for slot in range(near) for c in range(2)], axis=1)
         rhs = jnp.concatenate([basis[slot] for slot in range(near)], axis=0)
         total = jnp.dot(lhs, rhs, preferred_element_type=F32)
         for off in range(1, far):
             part_out[off - 1, at, :] = total[:, off * times:(off + 1) * times].astype(BF16)
-            rs_copy(off, chunk).start()
+            rs_copy(off, pl.ds(start, count), chunk).start()
         kept[at, :] = total[:, :times]
     for chunk, (start, count) in enumerate(chunks):
         at = slice(start, start + count)
         total = kept[at, :]
+        if far > 1:
+            rs_all(pl.ds(start, count), chunk).wait_recv()
         for off in range(1, far):
-            rs_copy(off, chunk).wait_recv()
             total = total + part_in[off - 1, at, :].astype(F32)
         out[at, :] = total * factor
-    for chunk in range(len(chunks)):
-        for off in range(1, near):
-            ag_copy(off, chunk).wait_send()
-        for off in range(1, far):
-            rs_copy(off, chunk).wait_send()
+    everything = pl.ds(0, here)
+    for off in range(1, depth_n):
+        pick_copy(off, everything, 0).wait_send()
+    if near > 1:
+        ag_all(everything, 0).wait_send()
+    if far > 1:
+        rs_all(everything, 0).wait_send()
 
 
 def local(depth_n, freq_n, pressure_field, block_main, block_coupled, coupling, frequencies,
@@ -363,20 +395,23 @@
     here = receivers.shape[0] // depth_n
     times = NT // freq_n
     factor = 1.0 / math.sqrt(frequencies.shape[0])
-    count = max(here // 4, 16)
-    chunks = [(start, count) for start in range(0, here, count)]
+    unit = here // 16
+    chunks = [(start * unit, size * unit) for start, size in CHUNKS]
     vmem = pl.BlockSpec(memory_space=pltpu.VMEM)
     hbm = pl.BlockSpec(memory_space=pltpu.HBM)
-    smem = pl.BlockSpec(memory_space=pltpu.SMEM)
     away = max(depth_n - 1, 1)
-    near_slots, far_slots = max(near - 1, 1), max(far - 1, 1)
+    far_slots = max(far - 1, 1)
     dma = pltpu.SemaphoreType.DMA
     return pl.pallas_call(
         functools.partial(kernel, depth_n, freq_n, near, factor, chunks),
         out_shape=jax.ShapeDtypeStruct((here, times), F32),
-        in_specs=[hbm, hbm, hbm, vmem, vmem, smem, smem],
+        in_specs=[hbm] * 7,
         out_specs=vmem,
         scratch_shapes=[
+            pltpu.VMEM((2, half), F32),
+            pltpu.VMEM((freq_n, half), F32),
+            pltpu.SMEM(receivers.shape, jnp.int32),
+            pltpu.SMEM(floors.shape, jnp.int32),
             pltpu.VMEM((rows, width), BF16),
             pltpu.VMEM((rows * KC, bs), BF16),
             pltpu.VMEM((rows * KC, bs), BF16),
@@ -386,23 +421,24 @@
             pltpu.VMEM((2, rows + 8, half), F32),
             pltpu.VMEM((STEPS, 2, 3, bs, half), BF16),
             pltpu.VMEM((depth_n, 2, here, half), F32),
-            pltpu.VMEM((away, len(chunks), 2, count, half), BF16),
-            pltpu.VMEM((away, len(chunks), 2, count, half), BF16),
-            pltpu.VMEM((near, len(chunks), 2, count, half), BF16),
+            pltpu.VMEM((away, 2, here, half), BF16),
+            pltpu.VMEM((away, 2, here, half), BF16),
+            pltpu.VMEM((near, 2, here, half), BF16),
             pltpu.VMEM((near, width, NT // near), BF16),
             pltpu.VMEM((here, times), F32),
             pltpu.VMEM((far_slots, here, times), BF16),
             pltpu.VMEM((far_slots, here, times), BF16),
-            dma((FIELD_PARTS,)),
+            dma((4,)),
+            dma(()),
             dma((2, len(group_cuts(nb)) - 1)),
-            dma((STEPS, 2)),
-            dma((STEPS, 2)),
+            dma((2, 2)),
+            dma((2, 2)),
+            dma((away,)),
             dma((away, len(chunks))),
-            dma((away, len(chunks))),
-            dma((near_slots, len(chunks))),
-            dma((near_slots, len(chunks))),
-            dma((far_slots, len(chunks))),
-            dma((far_slots, len(chunks))),
+            dma(()),
+            dma((len(chunks),)),
+            dma(()),
+            dma((len(chunks),)),
         ],
         compiler_params=pltpu.CompilerParams(
             collective_id=0, has_side_effects=True, vmem_limit_bytes=VMEM_LIMIT

time: 39.7 us -> 37.4 us (0.942)
  Pallas kernels: 38.9 us -> 36.6 us
    pallas_call x1, Pallas kernels: 38.9 us -> 36.6 us  [local(): pl.pallas_call(functools.partial(kernel, depth_n, freq_n, near, factor, c...]
where the time goes in v3:
time: 37.4 us; the launch traced here: 37.3 us
  Pallas kernels  36.6 us (98%)
  local copies, waits for them, and re-layouts  0.66 us (2%)
    pallas_call x1, Pallas kernels, local(): pl.pallas_call(functools.partial(kernel, depth_n, freq_n, near, factor, c...  36.6 us

profile of v3, /device:TPU:0, one launch (start us, length us, event | category | flops | bytes accessed | tf_op | source)
XLA Modules:
  0.0 37.3 jit_solution(11736362831257617590)
XLA Ops:
  0.0 36.6 %shard_map.73 = f32[256,128]{1,0:T(8,128)S(1)} custom-call(bf16[4096,256]{1,0:T(8,128)(2,1)} %field.1, bf16[24576,128]{1,0:T(8,128)(2,1)} %bitcast.4, bf16[24576,128]{1,0:T(8,128)(2,1)} %bitcast.5, f32[2,128]{1,0:T(2,128)} %bitcast.7, f32[16,128]{1,0:T(8,128)} %bitcast.6, s32[512]{0:T(512)} %receivers_hbm.1, s32[4]{0:T(128)} %floors_hbm.1), custom_call_target="tpu_custom_call" | custom-call | tf_op jit(solution)/shard_map/pallas_call | solution.py:405
  36.6 0.7 %copy.9 = f32[256,128]{1,0:T(8,128)} copy(f32[256,128]{1,0:T(8,128)S(1)} %shard_map.73) | data formatting | bytes 262144

commit v4 on v3

--- a/solution.py
+++ b/solution.py
@@ -23,7 +23,8 @@
 VMEM_LIMIT = 46 * 1024 * 1024
 GROUPS = (4, 8, 8, 8, 4)
 MEET = 3
-CHUNKS = ((0, 5), (5, 5), (10, 4), (14, 2))
+EXTRA = 5
+UNITS = 16
 AHEAD = 3
 FIELD_PARTS = 8
 
@@ -42,11 +43,11 @@
     return cuts
 
 
-def kernel(depth_n, freq_n, near, factor, chunks,
+def kernel(depth_n, freq_n, near, factor, chunks, extra,
            field, main_hbm, side_hbm, coupling_hbm, freqs_hbm, receivers_hbm, floors_hbm, out,
            coupling, freqs, receivers, floors, fbuf, raw_main, raw_side, ops, w_even, w_odd, final, halo, rows_f32, pick_out, pick_in,
            gathered, basis, kept, part_out, part_in,
-           small_sem, field_sem, load_sem, halo_send, halo_recv, pick_send, pick_recv, ag_send, ag_recv, rs_send, rs_recv):
+           result_out, result_in, result_send, result_recv, small_sem, field_sem, load_sem, halo_send, halo_recv, pick_send, pick_recv, ag_send, ag_recv, rs_send, rs_recv):
     rows, width = fbuf.shape
     half = width // 2
     nb, _, bw, bs = ops.shape
@@ -261,16 +262,26 @@
 
     limit = jnp.uint32(rows)
 
-    def pick(owner, dst, chunk):
-        start, count = chunks[chunk]
-
+    heavy, light = me_d == depth_n - 1, me_d == 0
+    shared = here - extra
+
+    def by(who, kind, body):
+        if kind == "both":
+            body()
+        else:
+            pl.when(who)(body)
+
+    def pick(base, dst, start, count):
         def one(j, carry):
-            spot = receivers[owner * here + start + j] - first_row
+            spot = receivers[base + j] - first_row
             spot = jnp.minimum(spot.astype(jnp.uint32), limit).astype(jnp.int32)
             for c in range(2):
                 dst[c, pl.ds(start + j, 1), :] = final[c, pl.ds(spot, 1), :]
             return carry
         lax.fori_loop(0, count, one, 0, unroll=16)
+
+    def base_of(kind, owner, start):
+        return shared if kind == "moved" else owner * here + start
 
     def pick_copy(off, at, chunk):
         return pltpu.make_async_remote_copy(
@@ -283,12 +294,16 @@
         )
 
     for off in range(1, depth_n):
-        for chunk, (start, count) in enumerate(chunks):
-            pick(lax.rem(me_d + off, depth_n), rows_f32.at[off], chunk)
-            pick_out[off - 1, :, start:start + count, :] = rows_f32[off, :, start:start + count, :].astype(BF16)
-            pick_copy(off, pl.ds(start, count), chunk).start()
-    for chunk in range(len(chunks)):
-        pick(me_d, rows_f32.at[0], chunk)
+        for chunk, (start, count, kind) in enumerate(chunks):
+            def give(off=off, chunk=chunk, start=start, count=count, kind=kind):
+                pick(base_of(kind, lax.rem(me_d + off, depth_n), start), rows_f32.at[off], start, count)
+                pick_out[off - 1, :, start:start + count, :] = rows_f32[off, :, start:start + count, :].astype(BF16)
+                pick_copy(off, pl.ds(start, count), chunk).start()
+            by(light, kind, give)
+    for chunk, (start, count, kind) in enumerate(chunks):
+        def take(start=start, count=count, kind=kind):
+            pick(base_of(kind, me_d, start), rows_f32.at[0], start, count)
+        by(heavy, kind, take)
 
     def ag_copy(off, at, chunk):
         return pltpu.make_async_remote_copy(
@@ -311,15 +326,17 @@
             device_id_type=MESH,
         )
 
-    for chunk, (start, count) in enumerate(chunks):
-        at = slice(start, start + count)
-        mine = rows_f32[0, :, at, :]
-        for off in range(1, depth_n):
-            pick_copy(off, pl.ds(start, count), chunk).wait_recv()
-            mine = mine + pick_in[off - 1, :, at, :].astype(F32)
-        gathered[0, :, at, :] = mine.astype(BF16)
-        for off in range(near - 1, 0, -1):
-            ag_copy(off, pl.ds(start, count), chunk).start()
+    for chunk, (start, count, kind) in enumerate(chunks):
+        def spread(chunk=chunk, start=start, count=count):
+            at = slice(start, start + count)
+            mine = rows_f32[0, :, at, :]
+            for off in range(1, depth_n):
+                pick_copy(off, pl.ds(start, count), chunk).wait_recv()
+                mine = mine + pick_in[off - 1, :, at, :].astype(F32)
+            gathered[0, :, at, :] = mine.astype(BF16)
+            for off in range(near - 1, 0, -1):
+                ag_copy(off, pl.ds(start, count), chunk).start()
+        by(heavy, kind, spread)
 
     lane = lax.broadcasted_iota(jnp.int32, (half, wide), 1)
     owner = lax.rem(lane // times + me_far, far)
@@ -356,32 +373,65 @@
             device_id_type=MESH,
         )
 
-    for chunk, (start, count) in enumerate(chunks):
-        at = slice(start, start + count)
+    for chunk, (start, count, kind) in enumerate(chunks):
+        def synthesize(chunk=chunk, start=start, count=count):
+            at = slice(start, start + count)
+            if near > 1:
+                ag_all(pl.ds(start, count), chunk).wait_recv()
+            lhs = jnp.concatenate([gathered[slot, c, at, :] for slot in range(near) for c in range(2)], axis=1)
+            rhs = jnp.concatenate([basis[slot] for slot in range(near)], axis=0)
+            total = jnp.dot(lhs, rhs, preferred_element_type=F32)
+            for off in range(1, far):
+                part_out[off - 1, at, :] = total[:, off * times:(off + 1) * times].astype(BF16)
+                rs_copy(off, pl.ds(start, count), chunk).start()
+            kept[at, :] = total[:, :times]
+        by(heavy, kind, synthesize)
+
+    result_copy = pltpu.make_async_remote_copy(
+        src_ref=result_out,
+        dst_ref=result_in,
+        send_sem=result_send,
+        recv_sem=result_recv,
+        device_id={"depth": 0},
+        device_id_type=MESH,
+    )
+    for chunk, (start, count, kind) in enumerate(chunks):
+        def finish(chunk=chunk, start=start, count=count, kind=kind):
+            at = slice(start, start + count)
+            total = kept[at, :]
+            if far > 1:
+                rs_all(pl.ds(start, count), chunk).wait_recv()
+            for off in range(1, far):
+                total = total + part_in[off - 1, at, :].astype(F32)
+            if kind == "moved":
+                result_out[...] = total * factor
+                result_copy.start()
+            else:
+                out[at, :] = total * factor
+        by(heavy, kind, finish)
+
+    def close(sent, owned):
+        for off in range(1, depth_n):
+            pick_copy(off, pl.ds(0, sent), 0).wait_send()
         if near > 1:
-            ag_all(pl.ds(start, count), chunk).wait_recv()
-        lhs = jnp.concatenate([gathered[slot, c, at, :] for slot in range(near) for c in range(2)], axis=1)
-        rhs = jnp.concatenate([basis[slot] for slot in range(near)], axis=0)
-        total = jnp.dot(lhs, rhs, preferred_element_type=F32)
-        for off in range(1, far):
-            part_out[off - 1, at, :] = total[:, off * times:(off + 1) * times].astype(BF16)
-            rs_copy(off, pl.ds(start, count), chunk).start()
-        kept[at, :] = total[:, :times]
-    for chunk, (start, count) in enumerate(chunks):
-        at = slice(start, start + count)
-        total = kept[at, :]
+            ag_all(pl.ds(0, owned), 0).wait_send()
         if far > 1:
-            rs_all(pl.ds(start, count), chunk).wait_recv()
-        for off in range(1, far):
-            total = total + part_in[off - 1, at, :].astype(F32)
-        out[at, :] = total * factor
-    everything = pl.ds(0, here)
-    for off in range(1, depth_n):
-        pick_copy(off, everything, 0).wait_send()
-    if near > 1:
-        ag_all(everything, 0).wait_send()
-    if far > 1:
-        rs_all(everything, 0).wait_send()
+            rs_all(pl.ds(0, owned), 0).wait_send()
+
+    if not extra:
+        close(here, here)
+        return
+
+    @pl.when(heavy)
+    def _():
+        result_copy.wait_send()
+        close(shared, here + extra)
+
+    @pl.when(light)
+    def _():
+        result_copy.wait_recv()
+        out[shared:, :] = result_in[...]
+        close(here + extra, shared)
 
 
 def local(depth_n, freq_n, pressure_field, block_main, block_coupled, coupling, frequencies,
@@ -395,15 +445,22 @@
     here = receivers.shape[0] // depth_n
     times = NT // freq_n
     factor = 1.0 / math.sqrt(frequencies.shape[0])
-    unit = here // 16
-    chunks = [(start * unit, size * unit) for start, size in CHUNKS]
+    unit = here // UNITS
+    extra = EXTRA * unit if depth_n == 2 else 0
+    room = here + extra
+    shared = (here - extra) // unit
+    cuts = [0, shared * 3 // 8, shared * 6 // 8, shared]
+    chunks = [(lo * unit, (hi - lo) * unit, "both") for lo, hi in zip(cuts, cuts[1:])]
+    if extra:
+        chunks.insert(1, (here, extra, "moved"))
+        chunks.insert(3, (here - extra, extra, "own"))
     vmem = pl.BlockSpec(memory_space=pltpu.VMEM)
     hbm = pl.BlockSpec(memory_space=pltpu.HBM)
     away = max(depth_n - 1, 1)
     far_slots = max(far - 1, 1)
     dma = pltpu.SemaphoreType.DMA
     return pl.pallas_call(
-        functools.partial(kernel, depth_n, freq_n, near, factor, chunks),
+        functools.partial(kernel, depth_n, freq_n, near, factor, chunks, extra),
         out_shape=jax.ShapeDtypeStruct((here, times), F32),
         in_specs=[hbm] * 7,
         out_specs=vmem,
@@ -420,14 +477,18 @@
             pltpu.VMEM((3, rows, half), BF16),
             pltpu.VMEM((2, rows + 8, half), F32),
             pltpu.VMEM((STEPS, 2, 3, bs, half), BF16),
-            pltpu.VMEM((depth_n, 2, here, half), F32),
-            pltpu.VMEM((away, 2, here, half), BF16),
-            pltpu.VMEM((away, 2, here, half), BF16),
-            pltpu.VMEM((near, 2, here, half), BF16),
+            pltpu.VMEM((depth_n, 2, room, half), F32),
+            pltpu.VMEM((away, 2, room, half), BF16),
+            pltpu.VMEM((away, 2, room, half), BF16),
+            pltpu.VMEM((near, 2, room, half), BF16),
             pltpu.VMEM((near, width, NT // near), BF16),
-            pltpu.VMEM((here, times), F32),
-            pltpu.VMEM((far_slots, here, times), BF16),
-            pltpu.VMEM((far_slots, here, times), BF16),
+            pltpu.VMEM((room, times), F32),
+            pltpu.VMEM((far_slots, room, times), BF16),
+            pltpu.VMEM((far_slots, room, times), BF16),
+            pltpu.VMEM((max(extra, 8), times), F32),
+            pltpu.VMEM((max(extra, 8), times), F32),
+            dma(()),
+            dma(()),
             dma((4,)),
             dma(()),
             dma((2, len(group_cuts(nb)) - 1)),

time: 37.4 us -> 36.3 us (0.971); the launches traced: 37.3 us -> 35.6 us
  Pallas kernels: 36.6 us -> 35 us
    pallas_call x1, Pallas kernels: 36.6 us -> 35 us  [local(): pl.pallas_call(functools.partial(kernel, depth_n, freq_n, near, factor, c...]
where the time goes in v4:
time: 36.3 us; the launch traced here: 35.6 us
  Pallas kernels  35 us (96%)
  local copies, waits for them, and re-layouts  0.66 us (2%)
    pallas_call x1, Pallas kernels, local(): pl.pallas_call(functools.partial(kernel, depth_n, freq_n, near, factor, c...  35 us

profile of v4, /device:TPU:0, one launch (start us, length us, event | category | flops | bytes accessed | tf_op | source)
XLA Modules:
  0.0 35.6 jit_solution(1877047009009285061)
XLA Ops:
  0.0 35.0 %shard_map.73 = f32[256,128]{1,0:T(8,128)S(1)} custom-call(bf16[4096,256]{1,0:T(8,128)(2,1)} %field.1, bf16[24576,128]{1,0:T(8,128)(2,1)} %bitcast.4, bf16[24576,128]{1,0:T(8,128)(2,1)} %bitcast.5, f32[2,128]{1,0:T(2,128)} %bitcast.7, f32[16,128]{1,0:T(8,128)} %bitcast.6, s32[512]{0:T(512)} %receivers_hbm.1, s32[4]{0:T(128)} %floors_hbm.1), custom_call_target="tpu_custom_call" | custom-call | tf_op jit(solution)/shard_map/pallas_call | solution.py:462
  35.0 0.7 %copy.9 = f32[256,128]{1,0:T(8,128)} copy(f32[256,128]{1,0:T(8,128)S(1)} %shard_map.73) | data formatting | bytes 262144

commit v5 on v4

--- a/solution.py
+++ b/solution.py
@@ -23,7 +23,7 @@
 VMEM_LIMIT = 46 * 1024 * 1024
 GROUPS = (4, 8, 8, 8, 4)
 MEET = 3
-EXTRA = 5
+EXTRA = 6
 UNITS = 16
 AHEAD = 3
 FIELD_PARTS = 8
@@ -449,7 +449,7 @@
     extra = EXTRA * unit if depth_n == 2 else 0
     room = here + extra
     shared = (here - extra) // unit
-    cuts = [0, shared * 3 // 8, shared * 6 // 8, shared]
+    cuts = [0, shared * 2 // 5, shared * 4 // 5, shared]
     chunks = [(lo * unit, (hi - lo) * unit, "both") for lo, hi in zip(cuts, cuts[1:])]
     if extra:
         chunks.insert(1, (here, extra, "moved"))

time: 36.3 us -> 36.3 us (level)
  no operation moved by 1% of the time
where the time goes in v5:
time: 36.3 us; the launch traced here: 35.6 us
  Pallas kernels  34.9 us (96%)
  local copies, waits for them, and re-layouts  0.66 us (2%)
    pallas_call x1, Pallas kernels, local(): pl.pallas_call(functools.partial(kernel, depth_n, freq_n, near, factor, c...  34.9 us

profile of v5, /device:TPU:0, one launch (start us, length us, event | category | flops | bytes accessed | tf_op | source)
XLA Modules:
  0.0 35.6 jit_solution(1189149474536112362)
XLA Ops:
  0.0 34.9 %shard_map.73 = f32[256,128]{1,0:T(8,128)S(1)} custom-call(bf16[4096,256]{1,0:T(8,128)(2,1)} %field.1, bf16[24576,128]{1,0:T(8,128)(2,1)} %bitcast.4, bf16[24576,128]{1,0:T(8,128)(2,1)} %bitcast.5, f32[2,128]{1,0:T(2,128)} %bitcast.7, f32[16,128]{1,0:T(8,128)} %bitcast.6, s32[512]{0:T(512)} %receivers_hbm.1, s32[4]{0:T(128)} %floors_hbm.1), custom_call_target="tpu_custom_call" | custom-call | tf_op jit(solution)/shard_map/pallas_call | solution.py:462
  34.9 0.7 %copy.9 = f32[256,128]{1,0:T(8,128)} copy(f32[256,128]{1,0:T(8,128)S(1)} %shard_map.73) | data formatting | bytes 262144
